TPU v7x, 128 devices: a whole 4x4x4 slice. The times are simulated.
128 devices in a mesh: team: 8 (over x, core), inner: 16 (over z, y).
Axes of the slice: x: 4, y: 4, z: 4, core: 2. Of those that a mesh axis runs over, the one named last changes fastest.
Arguments:
- queries: float32 [16384, 1024], P(('team', 'inner')), may hold values from -8 to 8
- passages: float32 [16384, 1024], P(('team', 'inner')), may hold values from -8 to 8
- positive: int32 [16384], P(('team', 'inner')), may hold values from 0 to 16383, as said below
Outputs:
- grad_queries: float32 [16384, 1024], P(('team', 'inner'))
- grad_passages: float32 [16384, 1024], P(('team', 'inner'))
Inputs may be any that keep to these rules, and one draw needn't show every extreme that they name: `positive`: a permutation of the passage indices 0 to 16383.
All inputs are finite; a program needn't handle non-finite values.
Results may differ from a plain program's by a relative error of at most 0.014.
Values may be sent and summed in bfloat16 or wider, within the bound.
A program may use at most 64 MiB of HBM per device.

v0:
```python
import jax
import jax.numpy as jnp
from jax import lax
from jax.sharding import Mesh
from jax.sharding import PartitionSpec as P

INNER = ("inner_0", "inner_1")
TEAM_INNER = ("team", "inner_0", "inner_1")
logit_scale_factor = 20.0
epsilon = 1e-06


def in_order(blocks, dim):
    dims = list(blocks.shape[1:])
    dims[dim] *= blocks.shape[0]
    return jnp.moveaxis(blocks, 0, dim).reshape(dims)


def sent_to_all(x, axis):
    copies = jnp.broadcast_to(x, (lax.axis_size(axis), *x.shape))
    return lax.all_to_all(copies, axis, split_axis=0, concat_axis=0, tiled=True)


def gathered_copies(x, axis, dim):
    return in_order(sent_to_all(x, axis), dim)


def taken_together(x, axis):
    everything = sent_to_all(x, axis)
    return jnp.sum(everything, axis=0)


def summed_rows(terms, axes):
    so_far = terms.astype(jnp.bfloat16)
    for axis in axes:
        so_far = lax.psum_scatter(so_far, axis, scatter_dimension=0, tiled=True)
    return so_far.astype(jnp.float32)


def split_up(x, dim, size):
    dims = x.shape
    blocks = x.reshape(*dims[:dim], size, dims[dim] // size, *dims[dim + 1 :])
    return jnp.moveaxis(blocks, dim, 0)


def summed_on_arrival(x, axis, dim):
    size = lax.axis_size(axis)
    blocks = lax.all_to_all(split_up(x, dim, size), axis, 0, 0, tiled=True)
    return jnp.sum(blocks.astype(jnp.float32), axis=0)


def unit_rows(vectors):
    length = jnp.sqrt(jnp.sum(vectors * vectors, axis=1, keepdims=True) + epsilon)
    return (vectors / length, length)


def finish(unit_vectors, length, grad_raw):
    projection = jnp.sum(unit_vectors * grad_raw, axis=1, keepdims=True)
    return (grad_raw - unit_vectors * projection) / length


def exponent(query_tile_rows, column_block):
    similarity_scores = lax.dot_general(
        query_tile_rows, column_block, (((1,), (1,)), ((), ())), preferred_element_type=jnp.float32
    )
    return jnp.exp(logit_scale_factor * similarity_scores)


def weights(query_tile_rows, column_block, target_block, row_block, column_block_total):
    exponentials = exponent(query_tile_rows, column_block)
    column_ids = lax.iota(jnp.int32, column_block.shape[0])
    is_target = (target_block[:, None] == column_ids[None, :]).astype(jnp.float32)
    combined = (
        exponentials / row_block[:, None]
        + exponentials / column_block_total[None, :]
        - 2.0 * is_target
    )
    return combined.astype(jnp.bfloat16)


def per_device(queries, passages, positive):
    shard_rows = queries.shape[0]
    feature_count = queries.shape[1]
    inner_count = lax.axis_size(INNER)
    team_count = lax.axis_size("team")
    query_unit, query_length = unit_rows(queries)
    passage_unit, passage_length = unit_rows(passages)
    query_round = query_unit.astype(jnp.bfloat16)
    passage_round = passage_unit.astype(jnp.bfloat16)
    team_queries = lax.all_gather(query_round, INNER, axis=0, tiled=True)
    team_targets = lax.all_gather(positive, INNER, axis=0, tiled=True)
    columns = gathered_copies(passage_round, "team", 0)
    team_rows = shard_rows * inner_count
    column_count = shard_rows * team_count
    owner_inner = team_targets % team_rows // shard_rows
    target_column = team_targets // team_rows * shard_rows + team_targets % shard_rows
    target_column = jnp.where(owner_inner == lax.axis_index(INNER), target_column, -1)
    block_rows = shard_rows * min(inner_count, max(1, 512 // shard_rows))
    block_count = team_rows // block_rows
    query_blocks = team_queries.reshape(block_count, block_rows, feature_count)

    def column_sums(running, query_tile_rows):
        exponentials = exponent(query_tile_rows, columns)
        return (running + jnp.sum(exponentials, axis=0), jnp.sum(exponentials, axis=1))

    column_part, row_parts = lax.scan(
        column_sums, jnp.zeros((column_count,), jnp.float32), query_blocks
    )
    row_total = taken_together(row_parts.reshape(team_rows), INNER)
    column_total = lax.psum(column_part, "team")
    query_tile_rows = team_queries
    loss_weight = weights(query_tile_rows, columns, target_column, row_total, column_total)
    query_grad = summed_rows(
        logit_scale_factor * jnp.dot(loss_weight, columns, preferred_element_type=jnp.float32),
        INNER,
    )
    loss_weight = weights(team_queries, columns, target_column, row_total, column_total)
    passage_grad = summed_on_arrival(
        (
            logit_scale_factor
            * lax.dot_general(
                loss_weight,
                team_queries,
                (((0,), (0,)), ((), ())),
                preferred_element_type=jnp.float32,
            )
        ).astype(jnp.bfloat16),
        "team",
        0,
    )
    grad_queries = finish(query_unit, query_length, query_grad)
    grad_passages = finish(passage_unit, passage_length, passage_grad)
    return (grad_queries, grad_passages)


def solution(mesh):
    finer = Mesh(mesh.devices.reshape(mesh.shape["team"], 4, 4), ("team", "inner_0", "inner_1"))
    in_specs = (P(TEAM_INNER, None), P(TEAM_INNER, None), P(TEAM_INNER))
    out_specs = (P(TEAM_INNER, None), P(TEAM_INNER, None))
    return jax.shard_map(
        per_device, mesh=finer, in_specs=in_specs, out_specs=out_specs, check_vma=False
    )
```

profile of v0, /device:TPU:0, one launch (start us, length us, event | category | flops | bytes accessed | tf_op | source)
XLA Modules:
  0.0 193.5 jit_solution(252195710733847977)
XLA Ops:
  7.2 0.0 all-gather.3.cloned.1.call-start
  7.2 1.2 multiply_reduce_fusion.2
  8.4 1.9 fusion.18
  10.2 0.0 copy-start.2
  10.2 0.0 all-gather.3.cloned.1.call-update
  10.3 1.2 multiply_reduce_fusion.1
  11.4 1.1 fusion.17
  12.6 1.6 broadcast_in_dim.16
  14.2 4.4 %all-to-all-start = ((bf16[8,128,1024]{2,1,0:T(8,128)(2,1)}), bf16[8,128,1024]{2,1,0:T(8,128)(2,1)S(1)}, u32[]{:S(2)}, u32[]{:S(2)}) async-start(bf16[8,128,1024]{2,1,0:T(8,128)(2,1)} %broadcast_in_dim.16), calls=%async_computation | async-start | bytes 4194304 | tf_op jit(solution)/shard_map/all_to_all | solution.py:21
  18.6 0.0 copy-done.2
  18.6 22.2 %all-gather = s32[16,1,128]{2,1,0:T(1,128)S(1)} all-gather(s32[1,1,128]{2,1,0:T(1,128)S(1)} %bitcast.32), channel_id=1, replica_groups=mesh['team'=8,'inner_0'=4,'inner_1'=4] {'inner_0','inner_1'}, dimensions={0}, use_global_device_ids=true | all-gather | bytes 8704 | tf_op jit(solution)/shard_map/all_gather | solution.py:91
  40.8 5.0 %all-to-all-done = bf16[8,128,1024]{2,1,0:T(8,128)(2,1)S(1)} async-done(((bf16[8,128,1024]{2,1,0:T(8,128)(2,1)}), bf16[8,128,1024]{2,1,0:T(8,128)(2,1)S(1)}, u32[]{:S(2)}, u32[]{:S(2)}) %all-to-all-start) | async-done | bytes 2097184 | tf_op jit(solution)/shard_map/all_to_all | solution.py:21
  45.8 19.0 %all-gather.3.cloned.1.call-done = bf16[2048,1024]{1,0:T(8,128)(2,1)} async-done(((bf16[128,1024]{1,0:T(8,128)(2,1)}), bf16[2048,1024]{1,0:T(8,128)(2,1)}) %all-gather.3.cloned.1.call-update) | async-done | bytes 4194320 | tf_op jit(solution)/shard_map/all_gather | solution.py:90
  64.7 11.1 %while.13 = (s32[]{:T(128)}, f32[1024]{0:T(1024)S(1)}, f32[4,512]{1,0:T(4,128)S(1)}, bf16[4,512,1024]{2,1,0:T(8,128)(2,1)}, bf16[1024,1024]{1,0:T(8,128)(2,1)S(1)}, /*index=5*/s32[]{:T(128)}, s32[]{:T(128)}) while((s32[]{:T(128)}, f32[1024]{0:T(1024)S(1)}, f32[4,512]{1,0:T(4,128)S(1)}, bf16[4,512,1024]{2,1,0:T(8,128)(2,1)}, ...), condition=%wide.region_5.6_spmd.clone, body=%wide.region_2.5_spmd.clone.sunk | while | flops 1075315200 | bytes 3168359 | solution.py:106
  64.7 2.7 %fusion.29 = (f32[512]{0:T(512)S(1)}, f32[1024]{0:T(1024)S(1)}) fusion(bf16[1024,1024]{1,0:T(8,128)(2,1)S(1)} %get-tuple-element.115, bf16[4,512,1024]{2,1,0:T(8,128)(2,1)} %get-tuple-element.114, s32[]{:T(128)S(6)} %copy.12), kind=kOutput, calls=%fused_computation.1.clone.1 | convolution fusion | flops 1075313152 | bytes 3151876 | tf_op jit(solution)/shard_map/while/body/eval_jaxpr/dot_general | solution.py:63
  67.5 0.1 dynamic_update_slice.6
  67.5 2.7 %fusion.29 = (f32[512]{0:T(512)S(1)}, f32[1024]{0:T(1024)S(1)}) fusion(bf16[1024,1024]{1,0:T(8,128)(2,1)S(1)} %get-tuple-element.115, bf16[4,512,1024]{2,1,0:T(8,128)(2,1)} %get-tuple-element.114, s32[]{:T(128)S(6)} %copy.12), kind=kOutput, calls=%fused_computation.1.clone.1 | convolution fusion | flops 1075313152 | bytes 3151876 | tf_op jit(solution)/shard_map/while/body/eval_jaxpr/dot_general | solution.py:63
  70.2 0.1 dynamic_update_slice.6
  70.3 2.7 %fusion.29 = (f32[512]{0:T(512)S(1)}, f32[1024]{0:T(1024)S(1)}) fusion(bf16[1024,1024]{1,0:T(8,128)(2,1)S(1)} %get-tuple-element.115, bf16[4,512,1024]{2,1,0:T(8,128)(2,1)} %get-tuple-element.114, s32[]{:T(128)S(6)} %copy.12), kind=kOutput, calls=%fused_computation.1.clone.1 | convolution fusion | flops 1075313152 | bytes 3151876 | tf_op jit(solution)/shard_map/while/body/eval_jaxpr/dot_general | solution.py:63
  73.0 0.1 dynamic_update_slice.6
  73.1 2.7 %fusion.29 = (f32[512]{0:T(512)S(1)}, f32[1024]{0:T(1024)S(1)}) fusion(bf16[1024,1024]{1,0:T(8,128)(2,1)S(1)} %get-tuple-element.115, bf16[4,512,1024]{2,1,0:T(8,128)(2,1)} %get-tuple-element.114, s32[]{:T(128)S(6)} %copy.12), kind=kOutput, calls=%fused_computation.1.clone.1 | convolution fusion | flops 1075313152 | bytes 3151876 | tf_op jit(solution)/shard_map/while/body/eval_jaxpr/dot_general | solution.py:63
  75.8 0.1 dynamic_update_slice.6
  75.9 0.7 broadcast_in_dim.36
  76.6 5.3 %all-to-all-start.1 = ((f32[16,1,2048]{2,1,0:T(1,128)}), f32[16,1,2048]{2,1,0:T(1,128)S(1)}, u32[]{:S(2)}, u32[]{:S(2)}) async-start(f32[16,1,2048]{2,1,0:T(1,128)} %broadcast_in_dim.36), calls=%async_computation.1 | async-start | bytes 262144 | tf_op jit(solution)/shard_map/all_to_all | solution.py:21
  81.9 0.0 reduce-scatter.3.cloned.1.call-start
  82.0 14.4 %psum.7 = f32[1024]{0:T(1024)S(1)} all-reduce(f32[1024]{0:T(1024)S(1)} %get-tuple-element.31), channel_id=1, replica_groups=mesh['team'=8,'inner_0'=4,'inner_1'=4] {'team'}, use_global_device_ids=true, to_apply=%region_7.8 | all-reduce | flops 1024 | bytes 8192 | tf_op jit(solution)/shard_map/psum | solution.py:110
  96.4 0.0 all-to-all-done.1
  96.4 0.1 reduce_sum.74
  96.5 7.9 %subtract_convert_fusion = bf16[2048,1024]{1,0:T(8,128)(2,1)S(1)} fusion(bf16[2048,1024]{1,0:T(8,128)(2,1)} %bitcast.34, bf16[1024,1024]{1,0:T(8,128)(2,1)S(1)} %get-tuple-element.125, s32[2048]{0:T(1024)S(1)} %fusion.12, f32[1024]{0:T(1024)S(1)} %psum.7, f32[2048]{0:T(1024)S(1)} %reduce_sum.74), kind=kOutput, calls=%fused_computation.9 | convolution fusion | flops 4311744512 | bytes 10506240 | tf_op jit(solution)/shard_map/dot_general | solution.py:63
  104.4 0.0 copy-start.3
  104.4 2.0 %copy-done.3 = bf16[2048,1024]{1,0:T(8,128)(2,1)} copy-done((bf16[2048,1024]{1,0:T(8,128)(2,1)}, bf16[2048,1024]{1,0:T(8,128)(2,1)S(1)}, u32[]{:S(2)}) %copy-start.3) | copy-done | bytes 4194328
  106.4 6.1 %multiply_convert_fusion = bf16[2048,1024]{1,0:T(8,128)(2,1)} fusion(bf16[2048,1024]{1,0:T(8,128)(2,1)S(1)} %subtract_convert_fusion, bf16[1024,1024]{1,0:T(8,128)(2,1)S(1)} %get-tuple-element.125), kind=kOutput, calls=%fused_computation.8 | convolution fusion | flops 4299161600 | bytes 10485760 | tf_op jit(solution)/shard_map/dot_general | solution.py:114
  112.5 0.0 reduce-scatter.3.cloned.1.call-update
  112.5 9.4 %multiply_convert_fusion.1 = bf16[1024,1024]{1,0:T(8,128)(2,1)} fusion(bf16[2048,1024]{1,0:T(8,128)(2,1)} %copy-done.3, bf16[2048,1024]{1,0:T(8,128)(2,1)} %bitcast.35), kind=kOutput, calls=%fused_computation.12 | convolution fusion | flops 4297064448 | bytes 10485760 | tf_op jit(solution)/shard_map/dot_general | solution.py:121
  121.9 3.7 %all-to-all-start.2 = ((bf16[8,128,1024]{2,1,0:T(8,128)(2,1)}), bf16[8,128,1024]{2,1,0:T(8,128)(2,1)S(1)}, u32[]{:S(2)}, u32[]{:S(2)}) async-start(bf16[8,128,1024]{2,1,0:T(8,128)(2,1)} %bitcast.27), calls=%async_computation.4 | async-start | bytes 4194304 | tf_op jit(solution)/shard_map/all_to_all | solution.py:48
  125.6 0.0 copy-start.1
  125.6 0.0 reduce-scatter.5.cloned.1.call-start
  125.7 32.5 %reduce-scatter.3.cloned.1.call-done = bf16[512,1024]{1,0:T(8,128)(2,1)} async-done(((bf16[2048,1024]{1,0:T(8,128)(2,1)}), bf16[512,1024]{1,0:T(8,128)(2,1)}) %reduce-scatter.3.cloned.1.call-update) | async-done | bytes 1048592 | tf_op jit(solution)/shard_map/reduce_scatter | solution.py:36
  158.2 0.0 reduce-scatter.5.cloned.1.call-update
  158.2 0.0 all-to-all-done.2
  158.2 0.4 convert_reduce_fusion
  158.6 0.0 copy-done
  158.6 0.2 multiply_reduce_fusion
  158.8 1.0 subtract_divide_fusion
  159.8 24.1 %reduce-scatter.5.cloned.1.call-done = bf16[128,1024]{1,0:T(8,128)(2,1)} async-done(((bf16[512,1024]{1,0:T(8,128)(2,1)}), bf16[128,1024]{1,0:T(8,128)(2,1)}) %reduce-scatter.5.cloned.1.call-update) | async-done | bytes 262160 | tf_op jit(solution)/shard_map/reduce_scatter | solution.py:36
  183.9 0.0 copy-done.1
  183.9 1.2 fusion.6
  185.1 1.9 fusion.7
  (11 shorter events, 0.1 us)
Async XLA Ops:
  7.2 57.6 %all-gather.3.cloned.1.call-start = ((), (), s32[]{:S(2)}) async-start(), calls=%async_computation.5 | async-start | bytes 4456448 | tf_op jit(solution)/shard_map/all_gather | solution.py:90
  10.2 8.4 %copy-start.2 = (s32[128]{0:T(128)S(1)}, s32[128]{0:T(128)}, u32[]{:S(2)}) copy-start(s32[128]{0:T(128)} %param.7) | copy-start | bytes 1540
  14.2 31.6 %all-to-all-start = ((bf16[8,128,1024]{2,1,0:T(8,128)(2,1)}), bf16[8,128,1024]{2,1,0:T(8,128)(2,1)S(1)}, u32[]{:S(2)}, u32[]{:S(2)}) async-start(bf16[8,128,1024]{2,1,0:T(8,128)(2,1)} %broadcast_in_dim.16), calls=%async_computation | async-start | bytes 4194304 | tf_op jit(solution)/shard_map/all_to_all | solution.py:21
  76.6 19.8 %all-to-all-start.1 = ((f32[16,1,2048]{2,1,0:T(1,128)}), f32[16,1,2048]{2,1,0:T(1,128)S(1)}, u32[]{:S(2)}, u32[]{:S(2)}) async-start(f32[16,1,2048]{2,1,0:T(1,128)} %broadcast_in_dim.36), calls=%async_computation.1 | async-start | bytes 262144 | tf_op jit(solution)/shard_map/all_to_all | solution.py:21
  81.9 76.3 %reduce-scatter.3.cloned.1.call-start = ((), (), s32[]{:S(2)}) async-start(), calls=%async_computation.6 | async-start | bytes 5242880 | tf_op jit(solution)/shard_map/reduce_scatter | solution.py:36
  104.4 2.0 %copy-start.3 = (bf16[2048,1024]{1,0:T(8,128)(2,1)}, bf16[2048,1024]{1,0:T(8,128)(2,1)S(1)}, u32[]{:S(2)}) copy-start(bf16[2048,1024]{1,0:T(8,128)(2,1)S(1)} %subtract_convert_fusion) | copy-start | bytes 12582916
  121.9 36.7 %copy-start = (f32[128,1024]{1,0:T(8,128)S(1)}, f32[128,1024]{1,0:T(8,128)}, u32[]{:S(2)}) copy-start(f32[128,1024]{1,0:T(8,128)} %param.6) | copy-start | bytes 1572868
  121.9 36.3 %all-to-all-start.2 = ((bf16[8,128,1024]{2,1,0:T(8,128)(2,1)}), bf16[8,128,1024]{2,1,0:T(8,128)(2,1)S(1)}, u32[]{:S(2)}, u32[]{:S(2)}) async-start(bf16[8,128,1024]{2,1,0:T(8,128)(2,1)} %bitcast.27), calls=%async_computation.4 | async-start | bytes 4194304 | tf_op jit(solution)/shard_map/all_to_all | solution.py:48
  125.6 58.3 %copy-start.1 = (f32[128,1024]{1,0:T(8,128)S(1)}, f32[128,1024]{1,0:T(8,128)}, u32[]{:S(2)}) copy-start(f32[128,1024]{1,0:T(8,128)} %param.5) | copy-start | bytes 1572868
  125.6 58.3 %reduce-scatter.5.cloned.1.call-start = ((), (), s32[]{:S(2)}) async-start(), calls=%async_computation.7 | async-start | bytes 1310720 | tf_op jit(solution)/shard_map/reduce_scatter | solution.py:36
Sparse Core Ops, SparseCore 0:
  10.7 54.0 all-gather.2
  112.6 45.5 reduce-scatter.2
  160.6 23.2 reduce-scatter.4
where the time goes:
time: 194 us
  waiting for transfers between devices  80.6 us (42%)
  blocking collectives  36.5 us (19%)
  matrix products  34.2 us (18%)
  between operations  13.9 us (7%)
  starting transfers between devices  13.6 us (7%)
  other arithmetic  10.1 us (5%)
  local copies, waits for them, and re-layouts  4.51 us (2%)
    reduce_scatter x2, waiting for transfers between devices, summed_rows(): so_far = lax.psum_scatter(so_far, axis, scatter_dimension=0, tiled=True)  56.6 us
    all_gather x1, blocking collectives, per_device(): team_targets = lax.all_gather(positive, INNER, axis=0, tiled=True)  22.2 us
    all_gather x1, waiting for transfers between devices, per_device(): team_queries = lax.all_gather(query_round, INNER, axis=0, tiled=True)  19 us
    dot_general x5, matrix products, exponent(): lax.dot_general(query_tile_rows, column_block, (((1,), (1,)), ((), ())),...  18.8 us
    psum x1, blocking collectives, per_device(): column_total = lax.psum(column_part, 'team')  14.4 us
    all_to_all x2, starting transfers between devices, sent_to_all(): return lax.all_to_all(copies, axis, split_axis=0, concat_axis=0, tiled=True)  9.7 us
    dot_general x1, matrix products, per_device(): lax.dot_general(loss_weight, team_queries, (((0,), (0,)), ((), ())), pref...  9.41 us
    dot_general x1, matrix products, per_device(): jnp.dot(loss_weight, columns, preferred_element_type=jnp.float32)  6.06 us
  transfers between devices with their start and end apart: 6, of which 4 were waited for; matrix products, arithmetic and copies ran while one was open for 8% of the time, Pallas kernels for 0%

commit v1 on v0

--- a/solution.py
+++ b/solution.py
@@ -107,7 +107,11 @@
         column_sums, jnp.zeros((column_count,), jnp.float32), query_blocks
     )
     row_total = taken_together(row_parts.reshape(team_rows), INNER)
-    column_total = lax.psum(column_part, "team")
+    column_total = column_part
+    for hop in (1, 2, 4):
+        column_total = column_total + lax.ppermute(
+            column_total, "team", [(dev, dev ^ hop) for dev in range(8)]
+        )
     query_tile_rows = team_queries
     loss_weight = weights(query_tile_rows, columns, target_column, row_total, column_total)
     query_grad = summed_rows(

time: 194 us -> 212 us (1.093)
  waiting for transfers between devices: 80.6 us -> 109 us
  blocking collectives: 36.5 us -> 20 us
  starting transfers between devices: 13.6 us -> 18.7 us
  matrix products: 34.2 us -> 37.6 us
    all_to_all x2, waiting for transfers between devices: 5 us -> 29.7 us  [sent_to_all(): return lax.all_to_all(copies, axis, split_axis=0, concat_axis=0, tiled=True)]
    psum x1 -> x0, blocking collectives: 14.4 us -> none  [per_device(): column_total = lax.psum(column_part, 'team')]
    ppermute x0 -> x3, starting transfers between devices: none -> 4.49 us  [per_device(): lax.ppermute(column_total, 'team', [(dev, dev ^ hop) for dev in range(8)])]
    ppermute x0 -> x3, waiting for transfers between devices: none -> 3.56 us  [per_device(): lax.ppermute(column_total, 'team', [(dev, dev ^ hop) for dev in range(8)])]
    dot_general x1, matrix products: 6.06 us -> 8.29 us  [per_device(): jnp.dot(loss_weight, columns, preferred_element_type=jnp.float32)]
  transfers between devices with their start and end apart: 6 -> 9, of which waited for: 4 -> 7; matrix products, arithmetic and copies ran while one was open for 8% -> 7% of each run, Pallas kernels for 0% -> 0%
where the time goes in v1:
time: 212 us
  waiting for transfers between devices  109 us (51%)
  matrix products  37.6 us (18%)
  blocking collectives  20 us (9%)
  starting transfers between devices  18.7 us (9%)
  between operations  13.8 us (7%)
  other arithmetic  10.1 us (5%)
  local copies, waits for them, and re-layouts  2.54 us (1%)
    reduce_scatter x2, waiting for transfers between devices, summed_rows(): so_far = lax.psum_scatter(so_far, axis, scatter_dimension=0, tiled=True)  56.5 us
    all_to_all x2, waiting for transfers between devices, sent_to_all(): return lax.all_to_all(copies, axis, split_axis=0, concat_axis=0, tiled=True)  29.7 us
    all_gather x1, blocking collectives, per_device(): team_targets = lax.all_gather(positive, INNER, axis=0, tiled=True)  20 us
    dot_general x5, matrix products, exponent(): lax.dot_general(query_tile_rows, column_block, (((1,), (1,)), ((), ())),...  19.9 us
    all_gather x1, waiting for transfers between devices, per_device(): team_queries = lax.all_gather(query_round, INNER, axis=0, tiled=True)  19 us
    all_to_all x2, starting transfers between devices, sent_to_all(): return lax.all_to_all(copies, axis, split_axis=0, concat_axis=0, tiled=True)  9.98 us
    dot_general x1, matrix products, per_device(): lax.dot_general(loss_weight, team_queries, (((0,), (0,)), ((), ())), pref...  9.41 us
    dot_general x1, matrix products, per_device(): jnp.dot(loss_weight, columns, preferred_element_type=jnp.float32)  8.29 us
  transfers between devices with their start and end apart: 9, of which 7 were waited for; matrix products, arithmetic and copies ran while one was open for 7% of the time, Pallas kernels for 0%

profile of v1, /device:TPU:0, one launch (start us, length us, event | category | flops | bytes accessed | tf_op | source)
XLA Modules:
  0.0 211.7 jit_solution(12258316440650528211)
XLA Ops:
  7.2 0.0 all-gather.3.cloned.1.call-start
  7.2 1.2 multiply_reduce_fusion.2
  8.4 1.9 fusion.18
  10.2 0.0 all-gather.3.cloned.1.call-update
  10.3 1.2 multiply_reduce_fusion.1
  11.4 1.1 fusion.17
  12.6 1.6 broadcast_in_dim.16
  14.2 4.4 %all-to-all-start = ((bf16[8,128,1024]{2,1,0:T(8,128)(2,1)}), bf16[8,128,1024]{2,1,0:T(8,128)(2,1)S(1)}, u32[]{:S(2)}, u32[]{:S(2)}) async-start(bf16[8,128,1024]{2,1,0:T(8,128)(2,1)} %broadcast_in_dim.16), calls=%async_computation | async-start | bytes 4194304 | tf_op jit(solution)/shard_map/all_to_all | solution.py:21
  18.6 27.2 %all-to-all-done = bf16[8,128,1024]{2,1,0:T(8,128)(2,1)S(1)} async-done(((bf16[8,128,1024]{2,1,0:T(8,128)(2,1)}), bf16[8,128,1024]{2,1,0:T(8,128)(2,1)S(1)}, u32[]{:S(2)}, u32[]{:S(2)}) %all-to-all-start) | async-done | bytes 2097184 | tf_op jit(solution)/shard_map/all_to_all | solution.py:21
  45.8 19.0 %all-gather.3.cloned.1.call-done = bf16[2048,1024]{1,0:T(8,128)(2,1)} async-done(((bf16[128,1024]{1,0:T(8,128)(2,1)}), bf16[2048,1024]{1,0:T(8,128)(2,1)}) %all-gather.3.cloned.1.call-update) | async-done | bytes 4194320 | tf_op jit(solution)/shard_map/all_gather | solution.py:90
  64.7 10.9 %while.13 = (s32[]{:T(128)}, f32[1024]{0:T(1024)S(1)}, f32[4,512]{1,0:T(4,128)S(1)}, bf16[4,512,1024]{2,1,0:T(8,128)(2,1)}, bf16[1024,1024]{1,0:T(8,128)(2,1)S(1)}, /*index=5*/s32[]{:T(128)}, s32[]{:T(128)}) while((s32[]{:T(128)}, f32[1024]{0:T(1024)S(1)}, f32[4,512]{1,0:T(4,128)S(1)}, bf16[4,512,1024]{2,1,0:T(8,128)(2,1)}, ...), condition=%wide.region_5.6_spmd.clone, body=%wide.region_2.5_spmd.clone.sunk | while | flops 1075315200 | bytes 3168359 | solution.py:106
  64.7 2.7 %fusion.29 = (f32[512]{0:T(512)S(1)}, f32[1024]{0:T(1024)S(1)}) fusion(bf16[1024,1024]{1,0:T(8,128)(2,1)S(1)} %get-tuple-element.115, bf16[4,512,1024]{2,1,0:T(8,128)(2,1)} %get-tuple-element.114, s32[]{:T(128)S(6)} %copy.12), kind=kOutput, calls=%fused_computation.1.clone.1 | convolution fusion | flops 1075313152 | bytes 3151876 | tf_op jit(solution)/shard_map/while/body/eval_jaxpr/dot_general | solution.py:63
  67.4 0.1 dynamic_update_slice.6
  67.5 2.7 %fusion.29 = (f32[512]{0:T(512)S(1)}, f32[1024]{0:T(1024)S(1)}) fusion(bf16[1024,1024]{1,0:T(8,128)(2,1)S(1)} %get-tuple-element.115, bf16[4,512,1024]{2,1,0:T(8,128)(2,1)} %get-tuple-element.114, s32[]{:T(128)S(6)} %copy.12), kind=kOutput, calls=%fused_computation.1.clone.1 | convolution fusion | flops 1075313152 | bytes 3151876 | tf_op jit(solution)/shard_map/while/body/eval_jaxpr/dot_general | solution.py:63
  70.1 0.1 dynamic_update_slice.6
  70.2 2.7 %fusion.29 = (f32[512]{0:T(512)S(1)}, f32[1024]{0:T(1024)S(1)}) fusion(bf16[1024,1024]{1,0:T(8,128)(2,1)S(1)} %get-tuple-element.115, bf16[4,512,1024]{2,1,0:T(8,128)(2,1)} %get-tuple-element.114, s32[]{:T(128)S(6)} %copy.12), kind=kOutput, calls=%fused_computation.1.clone.1 | convolution fusion | flops 1075313152 | bytes 3151876 | tf_op jit(solution)/shard_map/while/body/eval_jaxpr/dot_general | solution.py:63
  72.9 0.1 dynamic_update_slice.6
  72.9 2.7 %fusion.29 = (f32[512]{0:T(512)S(1)}, f32[1024]{0:T(1024)S(1)}) fusion(bf16[1024,1024]{1,0:T(8,128)(2,1)S(1)} %get-tuple-element.115, bf16[4,512,1024]{2,1,0:T(8,128)(2,1)} %get-tuple-element.114, s32[]{:T(128)S(6)} %copy.12), kind=kOutput, calls=%fused_computation.1.clone.1 | convolution fusion | flops 1075313152 | bytes 3151876 | tf_op jit(solution)/shard_map/while/body/eval_jaxpr/dot_general | solution.py:63
  75.6 0.1 dynamic_update_slice.6
  75.7 0.1 collective-permute-start
  75.8 1.2 collective-permute-done
  76.9 1.5 collective-permute-start.1
  78.4 0.0 copy-done.2
  78.4 20.0 %all-gather = s32[16,1,128]{2,1,0:T(1,128)S(1)} all-gather(s32[1,1,128]{2,1,0:T(1,128)S(1)} %bitcast.32), channel_id=1, replica_groups=mesh['team'=8,'inner_0'=4,'inner_1'=4] {'inner_0','inner_1'}, dimensions={0}, use_global_device_ids=true | all-gather | bytes 8704 | tf_op jit(solution)/shard_map/all_gather | solution.py:91
  98.4 0.7 broadcast_in_dim.36
  99.2 5.6 %all-to-all-start.1 = ((f32[16,1,2048]{2,1,0:T(1,128)}), f32[16,1,2048]{2,1,0:T(1,128)S(1)}, u32[]{:S(2)}, u32[]{:S(2)}) async-start(f32[16,1,2048]{2,1,0:T(1,128)} %broadcast_in_dim.36), calls=%async_computation.1 | async-start | bytes 262144 | tf_op jit(solution)/shard_map/all_to_all | solution.py:21
  104.7 0.0 reduce-scatter.3.cloned.1.call-start
  104.8 0.0 collective-permute-done.1
  104.8 2.9 %collective-permute-start.2 = (f32[1024]{0:T(1024)S(1)}, f32[1024]{0:T(1024)S(1)}, u32[]{:S(2)}, u32[]{:S(2)}) collective-permute-start(f32[1024]{0:T(1024)S(1)} %add.60), channel_id=1, source_target_pairs={{0,64},{16,80},{32,96},{48,112},{64,0},{80,16},{96,32},{112,48},{1... | collective-permute-start | bytes 12296 | tf_op jit(solution)/shard_map/ppermute | solution.py:112
  107.8 2.4 %collective-permute-done.2 = f32[1024]{0:T(1024)S(1)} collective-permute-done((f32[1024]{0:T(1024)S(1)}, f32[1024]{0:T(1024)S(1)}, u32[]{:S(2)}, u32[]{:S(2)}) %collective-permute-start.2) | collective-permute-done | bytes 4128 | tf_op jit(solution)/shard_map/ppermute | solution.py:112
  110.2 2.5 %all-to-all-done.1 = f32[16,1,2048]{2,1,0:T(1,128)S(1)} async-done(((f32[16,1,2048]{2,1,0:T(1,128)}), f32[16,1,2048]{2,1,0:T(1,128)S(1)}, u32[]{:S(2)}, u32[]{:S(2)}) %all-to-all-start.1) | async-done | bytes 131104 | tf_op jit(solution)/shard_map/all_to_all | solution.py:21
  112.7 0.1 reduce_sum.74
  112.8 9.3 %subtract_convert_fusion = bf16[2048,1024]{1,0:T(8,128)(2,1)} fusion(s32[2048]{0:T(1024)S(1)} %fusion.12, f32[1024]{0:T(1024)S(1)} %add.61, f32[2048]{0:T(1024)S(1)} %reduce_sum.74, bf16[2048,1024]{1,0:T(8,128)(2,1)} %bitcast.34, bf16[1024,1024]{1,0:T(8,128)(2,1)S(1)} %get-tuple-element.125), kind=kOutput, calls=%fused_computation.9 | convolution fusion | flops 4311744512 | bytes 10506240 | tf_op jit(solution)/shard_map/dot_general | solution.py:63
  122.1 8.3 %multiply_convert_fusion = bf16[2048,1024]{1,0:T(8,128)(2,1)} fusion(bf16[2048,1024]{1,0:T(8,128)(2,1)} %subtract_convert_fusion, bf16[1024,1024]{1,0:T(8,128)(2,1)S(1)} %get-tuple-element.125), kind=kOutput, calls=%fused_computation.8 | convolution fusion | flops 4299161600 | bytes 10485760 | tf_op jit(solution)/shard_map/dot_general | solution.py:118
  130.4 0.0 reduce-scatter.3.cloned.1.call-update
  130.4 9.4 %multiply_convert_fusion.1 = bf16[1024,1024]{1,0:T(8,128)(2,1)} fusion(bf16[2048,1024]{1,0:T(8,128)(2,1)} %subtract_convert_fusion, bf16[2048,1024]{1,0:T(8,128)(2,1)} %bitcast.35), kind=kOutput, calls=%fused_computation.12 | convolution fusion | flops 4297064448 | bytes 10485760 | tf_op jit(solution)/shard_map/dot_general | solution.py:125
  139.8 4.1 %all-to-all-start.2 = ((bf16[8,128,1024]{2,1,0:T(8,128)(2,1)}), bf16[8,128,1024]{2,1,0:T(8,128)(2,1)S(1)}, u32[]{:S(2)}, u32[]{:S(2)}) async-start(bf16[8,128,1024]{2,1,0:T(8,128)(2,1)} %bitcast.27), calls=%async_computation.4 | async-start | bytes 4194304 | tf_op jit(solution)/shard_map/all_to_all | solution.py:48
  143.9 0.0 reduce-scatter.5.cloned.1.call-start
  143.9 32.3 %reduce-scatter.3.cloned.1.call-done = bf16[512,1024]{1,0:T(8,128)(2,1)} async-done(((bf16[2048,1024]{1,0:T(8,128)(2,1)}), bf16[512,1024]{1,0:T(8,128)(2,1)}) %reduce-scatter.3.cloned.1.call-update) | async-done | bytes 1048592 | tf_op jit(solution)/shard_map/reduce_scatter | solution.py:36
  176.3 0.0 reduce-scatter.5.cloned.1.call-update
  176.3 0.0 all-to-all-done.2
  176.3 0.3 convert_reduce_fusion
  176.7 0.0 copy-done
  176.7 0.2 multiply_reduce_fusion
  176.9 1.0 subtract_divide_fusion
  177.9 24.2 %reduce-scatter.5.cloned.1.call-done = bf16[128,1024]{1,0:T(8,128)(2,1)} async-done(((bf16[512,1024]{1,0:T(8,128)(2,1)}), bf16[128,1024]{1,0:T(8,128)(2,1)}) %reduce-scatter.5.cloned.1.call-update) | async-done | bytes 262160 | tf_op jit(solution)/shard_map/reduce_scatter | solution.py:36
  202.1 1.2 fusion.6
  203.3 1.9 fusion.7
  (17 shorter events, 0.1 us)
Async XLA Ops:
  7.2 57.6 %all-gather.3.cloned.1.call-start = ((), (), s32[]{:S(2)}) async-start(), calls=%async_computation.5 | async-start | bytes 4456448 | tf_op jit(solution)/shard_map/all_gather | solution.py:90
  14.2 31.6 %all-to-all-start = ((bf16[8,128,1024]{2,1,0:T(8,128)(2,1)}), bf16[8,128,1024]{2,1,0:T(8,128)(2,1)S(1)}, u32[]{:S(2)}, u32[]{:S(2)}) async-start(bf16[8,128,1024]{2,1,0:T(8,128)(2,1)} %broadcast_in_dim.16), calls=%async_computation | async-start | bytes 4194304 | tf_op jit(solution)/shard_map/all_to_all | solution.py:21
  64.7 13.7 %copy-start.2 = (s32[128]{0:T(128)S(1)}, s32[128]{0:T(128)}, u32[]{:S(2)}) copy-start(s32[128]{0:T(128)} %param.7) | copy-start | bytes 1540
  75.7 1.2 collective-permute-start
  76.9 27.9 %collective-permute-start.1 = (f32[1024]{0:T(1024)S(1)}, f32[1024]{0:T(1024)S(1)}, u32[]{:S(2)}, u32[]{:S(2)}) collective-permute-start(f32[1024]{0:T(1024)S(1)} %add.59), channel_id=1, source_target_pairs={{0,32},{16,48},{32,0},{48,16},{64,96},{80,112},{96,64},{112,80},{1... | collective-permute-start | bytes 12296 | tf_op jit(solution)/shard_map/ppermute | solution.py:112
  99.2 13.6 %all-to-all-start.1 = ((f32[16,1,2048]{2,1,0:T(1,128)}), f32[16,1,2048]{2,1,0:T(1,128)S(1)}, u32[]{:S(2)}, u32[]{:S(2)}) async-start(f32[16,1,2048]{2,1,0:T(1,128)} %broadcast_in_dim.36), calls=%async_computation.1 | async-start | bytes 262144 | tf_op jit(solution)/shard_map/all_to_all | solution.py:21
  104.7 71.5 %reduce-scatter.3.cloned.1.call-start = ((), (), s32[]{:S(2)}) async-start(), calls=%async_computation.6 | async-start | bytes 5242880 | tf_op jit(solution)/shard_map/reduce_scatter | solution.py:36
  104.8 5.4 %collective-permute-start.2 = (f32[1024]{0:T(1024)S(1)}, f32[1024]{0:T(1024)S(1)}, u32[]{:S(2)}, u32[]{:S(2)}) collective-permute-start(f32[1024]{0:T(1024)S(1)} %add.60), channel_id=1, source_target_pairs={{0,64},{16,80},{32,96},{48,112},{64,0},{80,16},{96,32},{112,48},{1... | collective-permute-start | bytes 12296 | tf_op jit(solution)/shard_map/ppermute | solution.py:112
  139.8 36.9 %copy-start = (f32[128,1024]{1,0:T(8,128)S(1)}, f32[128,1024]{1,0:T(8,128)}, u32[]{:S(2)}) copy-start(f32[128,1024]{1,0:T(8,128)} %param.6) | copy-start | bytes 1572868
  139.8 36.5 %all-to-all-start.2 = ((bf16[8,128,1024]{2,1,0:T(8,128)(2,1)}), bf16[8,128,1024]{2,1,0:T(8,128)(2,1)S(1)}, u32[]{:S(2)}, u32[]{:S(2)}) async-start(bf16[8,128,1024]{2,1,0:T(8,128)(2,1)} %bitcast.27), calls=%async_computation.4 | async-start | bytes 4194304 | tf_op jit(solution)/shard_map/all_to_all | solution.py:48
  143.9 58.2 %copy-start.1 = (f32[128,1024]{1,0:T(8,128)S(1)}, f32[128,1024]{1,0:T(8,128)}, u32[]{:S(2)}) copy-start(f32[128,1024]{1,0:T(8,128)} %param.5) | copy-start | bytes 1572868
  143.9 58.2 %reduce-scatter.5.cloned.1.call-start = ((), (), s32[]{:S(2)}) async-start(), calls=%async_computation.7 | async-start | bytes 1310720 | tf_op jit(solution)/shard_map/reduce_scatter | solution.py:36
Sparse Core Ops, SparseCore 0:
  10.7 53.9 all-gather.2
  130.5 45.7 reduce-scatter.2
  178.7 23.3 reduce-scatter.4
